TPU v7x, 32 devices: a whole 2x2x4 slice. The times are simulated.
32 devices in a mesh: replica: 8 (over z, y), shard: 4 (over x, core).
Axes of the slice: x: 2, y: 2, z: 4, core: 2. Of those that a mesh axis runs over, the one named last changes fastest.
Arguments:
- outer_params: float32 [512, 4096], P('shard'), may hold values from -6 to 6, as said below
- local_params: bfloat16 [8, 512, 4096], P('replica', 'shard'), may hold values from -70 to 70
- momentum: float32 [512, 4096], P('shard'), may hold values from -6 to 6
Outputs:
- params_next: float32 [512, 4096], P('shard')
- momentum_next: float32 [512, 4096], P('shard')
- block_scales: float32 [32, 512], P(None, 'shard')
Inputs may be any that keep to these rules, and one draw needn't show every extreme that they name: `outer_params`: outer parameters of order one.
All inputs are finite; a program needn't handle non-finite values.
Results may differ from a plain program's by a relative error of at most 0.005.
Values may be sent and summed in bfloat16 or wider, within the bound.
A program may use at most 64 MiB of HBM per device.

v0:
```python
import math
import jax
import jax.numpy as jnp
from jax import lax
from jax.sharding import PartitionSpec as P

BLOCK = 128
epsilon = 1e-06
clip_level = 0.5
outer_rate = 0.7
outer_decay = 0.9
grid_levels = 7.0


def smooth_step(values):
    return values - jnp.sin(2.0 * math.pi * values) / (2.0 * math.pi)


def smooth_round(values):
    return smooth_step(smooth_step(values))


def block_max(values):
    return jnp.max(
        jnp.abs(values).reshape(values.shape[0], values.shape[1] // BLOCK, BLOCK), axis=2
    )


def per_device(outer_params, local_params, momentum):
    workers = lax.axis_size("replica")
    row_count = outer_params.shape[0]
    col_count = outer_params.shape[1]
    slice_rows = row_count // workers
    slice_start = lax.axis_index("replica") * slice_rows
    deltas = outer_params - local_params[0].astype(jnp.float32)
    absmax = lax.pmax(block_max(deltas), "replica")
    spread_scale = jnp.repeat(absmax + epsilon, BLOCK, axis=1)
    encoded = smooth_round(grid_levels * deltas / spread_scale).astype(jnp.bfloat16)
    arrived = lax.all_to_all(encoded[None], "replica", split_axis=1, concat_axis=0, tiled=True)
    slice_scale = lax.dynamic_slice_in_dim(spread_scale, slice_start, slice_rows, 0)
    summed_rows = jnp.sum(arrived.astype(jnp.float32), axis=0) * slice_scale / grid_levels
    gradient_slice = summed_rows / workers
    square_total = lax.psum(jnp.sum(gradient_slice * gradient_slice), ("replica", "shard"))
    entry_count = row_count * lax.axis_size("shard") * col_count
    root_mean = jnp.sqrt(square_total / entry_count + epsilon)
    factor = jnp.minimum(1.0, clip_level / root_mean)
    gradient = lax.all_gather(gradient_slice, "replica", axis=0, tiled=True)
    clipped = factor * gradient
    momentum_next = outer_decay * momentum + clipped
    params_next = outer_params - outer_rate * (clipped + outer_decay * momentum_next)
    return (params_next, momentum_next, absmax.T)


def solution(mesh):
    return jax.shard_map(
        per_device,
        mesh=mesh,
        in_specs=(P("shard", None), P("replica", "shard", None), P("shard", None)),
        out_specs=(P("shard", None), P("shard", None), P(None, "shard")),
        check_vma=False,
    )
```

profile of v0, /device:TPU:0, one launch (start us, length us, event | category | flops | bytes accessed | tf_op | source)
XLA Modules:
  0.0 172.0 jit_solution(18044409390670645208)
XLA Ops:
  7.2 2.1 %abs_bitcast_fusion = f32[16,8,32,128]{3,1,2,0:T(8,128)S(1)} fusion(f32[128,4096]{1,0:T(8,128)} %param.3, bf16[1,128,4096]{2,1,0:T(8,128)(2,1)} %param.4), kind=kLoop, calls=%fused_computation.5 | loop fusion | flops 1572864 | bytes 5242880
  9.3 0.4 copy.11
  9.7 0.0 copy-start.1
  9.7 0.6 reduce_max.9
  10.3 39.3 %pmax.7 = f32[128,32]{1,0:T(8,128)S(1)} all-reduce(f32[128,32]{1,0:T(8,128)S(1)} %reduce_max.9), channel_id=1, replica_groups=mesh['replica'=8,'shard'=4] {'replica'}, use_global_device_ids=true, to_apply=%region_1.0 | all-reduce | flops 4096 | bytes 32768 | tf_op jit(solution)/shard_map/pmax | solution.py:36
  49.6 0.6 broadcast_in_dim.6
  50.2 15.9 %fusion = bf16[1,128,4096]{2,1,0:T(8,128)(2,1)S(1)} fusion(f32[128,4096]{1,0:T(8,128)} %param.3, bf16[1,128,4096]{2,1,0:T(8,128)(2,1)S(1)} %copy-done.1, f32[16,8,32,128]{3,2,1,0:T(8,128)S(1)} %bitcast.23), kind=kLoop, calls=%fused_computation.6 | loop fusion | flops 5767168 | bytes 6291456 | tf_op jit(solution)/shard_map/broadcast_in_dim | solution.py:39
  66.1 3.7 %copy.18 = bf16[1,128,4096]{2,0,1:T(2,128)(2,1)} copy(bf16[1,128,4096]{2,1,0:T(8,128)(2,1)S(1)} %fusion) | data formatting | bytes 2097152 | tf_op jit(solution)/shard_map/broadcast_in_dim | solution.py:39
  69.8 0.5 broadcast.25
  70.3 8.4 %reduce = bf16[128,4096]{1,0:T(8,128)(2,1)S(1)} reduce(bf16[128,1,4096]{2,1,0:T(2,128)(2,1)} %bitcast.26, bf16[]{:T(256)} %broadcast.25), dimensions={1}, to_apply=%bitcast.22.reduce_sub_computation | reduce | bytes 2097154
  78.7 1.6 reshape.23
  80.3 3.6 %all-to-all-start = ((bf16[8,2,32768]{2,1,0:T(2,128)(2,1)}), bf16[8,2,32768]{2,1,0:T(2,128)(2,1)S(1)}, u32[]{:S(2)}, u32[]{:S(2)}) async-start(bf16[8,2,32768]{2,1,0:T(2,128)(2,1)} %reshape.23), calls=%async_computation | async-start | bytes 2097152 | tf_op jit(solution)/shard_map/all_to_all | solution.py:39
  83.8 0.2 all-gather.2.cloned.1.call-start
  84.1 3.0 %copy.17 = f32[16,8,32,128]{3,1,2,0:T(8,128)} copy(f32[16,8,32,128]{3,2,1,0:T(8,128)S(1)} %bitcast.24) | data formatting | bytes 4194304
  87.0 15.8 %all-to-all-done = bf16[8,2,32768]{2,1,0:T(2,128)(2,1)S(1)} async-done(((bf16[8,2,32768]{2,1,0:T(2,128)(2,1)}), bf16[8,2,32768]{2,1,0:T(2,128)(2,1)S(1)}, u32[]{:S(2)}, u32[]{:S(2)}) %all-to-all-start) | async-done | bytes 1048608 | tf_op jit(solution)/shard_map/all_to_all | solution.py:39
  102.8 1.0 reshape.24
  103.8 3.0 %copy.10 = f32[1,128,4096]{2,1,0:T(8,128)} copy(bf16[1,128,4096]{2,0,1:T(2,128)(2,1)S(1)} %bitcast.28) | data formatting | bytes 3145728
  106.8 1.9 %reduce_sum.18 = f32[16,4096]{1,0:T(8,128)S(1)} reduce(f32[8,16,4096]{2,1,0:T(8,128)} %bitcast.25, f32[]{:T(128)} %constant.13.clone.1), dimensions={0}, to_apply=%region_2.0 | reduce | flops 458752 | bytes 2359300 | tf_op jit(solution)/shard_map/reduce_sum | solution.py:41
  108.7 2.3 %multiply_reduce_fusion = (f32[]{:T(128)}, f32[16,4096]{1,0:T(8,128)}) fusion(f32[16,4096]{1,0:T(8,128)S(1)} %reduce_sum.18, f32[128,4096]{1,0:T(8,128)} %bitcast.29, s32[]{:T(128)S(6)} %select_n.3), kind=kLoop, calls=%fused_computation.7 | loop fusion | flops 262143 | bytes 786440 | tf_op jit(solution)/shard_map/reduce_sum | solution.py:43
  111.0 0.0 all-gather.2.cloned.1.call-update
  111.0 0.7 copy.9
  111.7 39.4 %psum.7 = f32[]{:T(128)} all-reduce(f32[]{:T(128)} %get-tuple-element.11), channel_id=1, replica_groups=mesh['replica'=8,'shard'=4] {'replica','shard'}, use_global_device_ids=true, to_apply=%region_4.0 | all-reduce | flops 1 | bytes 8 | tf_op jit(solution)/shard_map/psum | solution.py:43
  151.7 8.5 %all-gather.2.cloned.1.call-done = f32[128,4096]{1,0:T(8,128)} async-done(((f32[16,4096]{1,0:T(8,128)}), f32[128,4096]{1,0:T(8,128)}) %all-gather.2.cloned.1.call-update) | async-done | bytes 2097168 | tf_op jit(solution)/shard_map/all_gather | solution.py:47
  160.2 4.9 %multiply_subtract_fusion = (f32[128,4096]{1,0:T(8,128)}, f32[128,4096]{1,0:T(8,128)}) fusion(f32[128,4096]{1,0:T(8,128)S(1)} %copy-done, f32[128,4096]{1,0:T(8,128)} %all-gather.2.cloned.1.call-done, f32[]{:T(128)S(6)} %min_shard_map.3, f32[128,4096]{1,0:T(8,128)} %param.5), kind=kLoop, calls=%fused_computation.2 | loop fusion | flops 3670016 | bytes 10485764 | tf_op jit(solution)/shard_map/sub | solution.py:50
  (4 shorter events, 0.0 us)
Async XLA Ops:
  9.7 40.6 %copy-start.1 = (bf16[1,128,4096]{2,1,0:T(8,128)(2,1)S(1)}, bf16[1,128,4096]{2,1,0:T(8,128)(2,1)}, u32[]{:S(2)}) copy-start(bf16[1,128,4096]{2,1,0:T(8,128)(2,1)} %param.4) | copy-start | bytes 3145732
  80.3 22.5 %all-to-all-start = ((bf16[8,2,32768]{2,1,0:T(2,128)(2,1)}), bf16[8,2,32768]{2,1,0:T(2,128)(2,1)S(1)}, u32[]{:S(2)}, u32[]{:S(2)}) async-start(bf16[8,2,32768]{2,1,0:T(2,128)(2,1)} %reshape.23), calls=%async_computation | async-start | bytes 2097152 | tf_op jit(solution)/shard_map/all_to_all | solution.py:39
  83.8 76.4 %all-gather.2.cloned.1.call-start = ((), (), s32[]{:S(2)}) async-start(), calls=%async_computation.1 | async-start | bytes 2359296 | tf_op jit(solution)/shard_map/all_gather | solution.py:47
  106.8 53.4 %copy-start = (f32[128,4096]{1,0:T(8,128)S(1)}, f32[128,4096]{1,0:T(8,128)}, u32[]{:S(2)}) copy-start(f32[128,4096]{1,0:T(8,128)} %param.3) | copy-start | bytes 6291460
Sparse Core Ops, SparseCore 0:
  111.1 49.0 all-gather.1
where the time goes:
time: 172 us
  blocking collectives  78.7 us (46%)
  other arithmetic  36 us (21%)
  waiting for transfers between devices  24.3 us (14%)
  between operations  14.8 us (9%)
  local copies, waits for them, and re-layouts  14.4 us (8%)
  starting transfers between devices  3.78 us (2%)
    psum x1, blocking collectives, per_device(): lax.psum(jnp.sum(gradient_slice * gradient_slice), ('replica', 'shard'))  39.4 us
    pmax x1, blocking collectives, per_device(): absmax = lax.pmax(block_max(deltas), 'replica')  39.3 us
    broadcast_in_dim x1, other arithmetic, per_device(): encoded[None]  15.9 us
    all_to_all x1, waiting for transfers between devices, per_device(): lax.all_to_all(encoded[None], 'replica', split_axis=1, concat_axis=0, til...  15.8 us
    unnamed x2, other arithmetic  10.5 us
    unnamed x11, local copies, waits for them, and re-layouts  10.1 us
    all_gather x1, waiting for transfers between devices, per_device(): gradient = lax.all_gather(gradient_slice, 'replica', axis=0, tiled=True)  8.49 us
    sub x1, other arithmetic, per_device(): outer_params - outer_rate * (clipped + outer_decay * momentum_next)  4.9 us
  transfers between devices with their start and end apart: 2, of which 2 were waited for; matrix products, arithmetic and copies ran while one was open for 2% of the time, Pallas kernels for 0%

commit v1 on v0

--- a/solution.py
+++ b/solution.py
@@ -36,7 +36,12 @@
     absmax = lax.pmax(block_max(deltas), "replica")
     spread_scale = jnp.repeat(absmax + epsilon, BLOCK, axis=1)
     encoded = smooth_round(grid_levels * deltas / spread_scale).astype(jnp.bfloat16)
-    arrived = lax.all_to_all(encoded[None], "replica", split_axis=1, concat_axis=0, tiled=True)
+    arrived = jnp.concatenate(
+        lax.all_to_all(
+            jnp.stack(jnp.split(encoded[None], lax.axis_size("replica"), axis=1)), "replica", 0, 0
+        ),
+        axis=0,
+    )
     slice_scale = lax.dynamic_slice_in_dim(spread_scale, slice_start, slice_rows, 0)
     summed_rows = jnp.sum(arrived.astype(jnp.float32), axis=0) * slice_scale / grid_levels
     gradient_slice = summed_rows / workers

time: 172 us -> 158 us (0.919)
  other arithmetic: 36 us -> 25.9 us
  local copies, waits for them, and re-layouts: 14.4 us -> 9.93 us
    unnamed x2 -> x1, other arithmetic: 10.5 us -> 2.11 us
    broadcast_in_dim x1 -> x0, local copies, waits for them, and re-layouts: 3.68 us -> none  [per_device(): encoded[None]]
    reduce_sum x1, other arithmetic: 1.86 us -> 0.14 us  [per_device(): jnp.sum(arrived.astype(jnp.float32), axis=0) * slice_scale / grid_levels]
    unnamed x11 -> x14, local copies, waits for them, and re-layouts: 10.1 us -> 8.66 us
where the time goes in v1:
time: 158 us; the launch traced here: 157 us
  blocking collectives  78.7 us (50%)
  other arithmetic  25.9 us (16%)
  waiting for transfers between devices  24.5 us (16%)
  between operations  14.8 us (9%)
  local copies, waits for them, and re-layouts  9.93 us (6%)
  starting transfers between devices  3.6 us (2%)
    psum x1, blocking collectives, per_device(): lax.psum(jnp.sum(gradient_slice * gradient_slice), ('replica', 'shard'))  39.4 us
    pmax x1, blocking collectives, per_device(): absmax = lax.pmax(block_max(deltas), 'replica')  39.3 us
    all_to_all x1, waiting for transfers between devices, per_device(): lax.all_to_all(jnp.stack(jnp.split(encoded[None], lax.axis_size('replica'...  16 us
    broadcast_in_dim x1, other arithmetic, per_device(): encoded[None]  15.9 us
    unnamed x14, local copies, waits for them, and re-layouts  8.66 us
    all_gather x1, waiting for transfers between devices, per_device(): gradient = lax.all_gather(gradient_slice, 'replica', axis=0, tiled=True)  8.49 us
    sub x1, other arithmetic, per_device(): outer_params - outer_rate * (clipped + outer_decay * momentum_next)  4.9 us
    all_to_all x1, starting transfers between devices, per_device(): lax.all_to_all(jnp.stack(jnp.split(encoded[None], lax.axis_size('replica'...  3.56 us
  transfers between devices with their start and end apart: 2, of which 2 were waited for; matrix products, arithmetic and copies ran while one was open for 2% of the time, Pallas kernels for 0%

profile of v1, /device:TPU:0, one launch (start us, length us, event | category | flops | bytes accessed | tf_op | source)
XLA Modules:
  0.0 157.4 jit_solution(7219774458395003367)
XLA Ops:
  7.2 2.1 %abs_bitcast_fusion = f32[16,8,32,128]{3,1,2,0:T(8,128)S(1)} fusion(f32[128,4096]{1,0:T(8,128)} %param.3, bf16[1,128,4096]{2,1,0:T(8,128)(2,1)} %param.4), kind=kLoop, calls=%fused_computation.6 | loop fusion | flops 1572864 | bytes 5242880
  9.3 0.4 copy.8
  9.7 0.6 reduce_max.9
  10.3 39.3 %pmax.7 = f32[128,32]{1,0:T(8,128)S(1)} all-reduce(f32[128,32]{1,0:T(8,128)S(1)} %reduce_max.9), channel_id=1, replica_groups=mesh['replica'=8,'shard'=4] {'replica'}, use_global_device_ids=true, to_apply=%region_1.0 | all-reduce | flops 4096 | bytes 32768 | tf_op jit(solution)/shard_map/pmax | solution.py:36
  49.6 0.6 broadcast_in_dim.6
  50.2 15.9 %fusion = bf16[1,128,4096]{2,1,0:T(8,128)(2,1)S(1)} fusion(f32[128,4096]{1,0:T(8,128)} %param.3, bf16[1,128,4096]{2,1,0:T(8,128)(2,1)S(1)} %copy-done.1, f32[16,8,32,128]{3,2,1,0:T(8,128)S(1)} %bitcast.50), kind=kLoop, calls=%fused_computation.7 | loop fusion | flops 5767168 | bytes 6291456 | tf_op jit(solution)/shard_map/broadcast_in_dim | solution.py:41
  66.1 0.7 fusion.8
  66.8 0.7 fusion.7
  67.4 0.7 fusion.6
  68.1 0.7 fusion.5
  68.8 0.7 fusion.4
  69.4 0.7 fusion.3
  70.1 0.7 fusion.2
  70.8 0.7 fusion.1
  71.4 3.6 %all-to-all-start = ((bf16[8,1,16,4096]{3,2,1,0:T(8,128)(2,1)}), bf16[8,1,16,4096]{3,2,1,0:T(8,128)(2,1)S(1)}, u32[]{:S(2)}, u32[]{:S(2)}) async-start(bf16[8,1,16,4096]{3,2,1,0:T(8,128)(2,1)} %fusion.1), calls=%async_computation | async-start | bytes 2097152 | tf_op jit(solution)/shard_map/all_to_all | solution.py:40
  75.0 0.0 all-gather.2.cloned.1.call-start
  75.0 3.0 %copy.13 = f32[16,8,32,128]{3,1,2,0:T(8,128)} copy(f32[16,8,32,128]{3,2,1,0:T(8,128)S(1)} %bitcast.51) | data formatting | bytes 4194304
  78.0 16.0 %all-to-all-done = bf16[8,1,16,4096]{3,2,1,0:T(8,128)(2,1)S(1)} async-done(((bf16[8,1,16,4096]{3,2,1,0:T(8,128)(2,1)}), bf16[8,1,16,4096]{3,2,1,0:T(8,128)(2,1)S(1)}, u32[]{:S(2)}, u32[]{:S(2)}) %all-to-all-start) | async-done | bytes 1048608 | tf_op jit(solution)/shard_map/all_to_all | solution.py:40
  94.0 0.1 convert_reduce_fusion
  94.1 2.3 %multiply_reduce_fusion = (f32[]{:T(128)}, f32[16,4096]{1,0:T(8,128)}) fusion(f32[16,4096]{1,0:T(8,128)S(1)} %convert_reduce_fusion, f32[128,4096]{1,0:T(8,128)} %bitcast.53, s32[]{:T(128)S(6)} %select_n.3), kind=kLoop, calls=%fused_computation.8 | loop fusion | flops 262143 | bytes 786440 | tf_op jit(solution)/shard_map/reduce_sum | solution.py:48
  96.4 0.7 copy.7
  97.1 39.4 %psum.7 = f32[]{:T(128)} all-reduce(f32[]{:T(128)} %get-tuple-element.8), channel_id=1, replica_groups=mesh['replica'=8,'shard'=4] {'replica','shard'}, use_global_device_ids=true, to_apply=%region_4.0 | all-reduce | flops 1 | bytes 8 | tf_op jit(solution)/shard_map/psum | solution.py:48
  137.1 8.5 %all-gather.2.cloned.1.call-done = f32[128,4096]{1,0:T(8,128)} async-done(((f32[16,4096]{1,0:T(8,128)}), f32[128,4096]{1,0:T(8,128)}) %all-gather.2.cloned.1.call-update) | async-done | bytes 2097168 | tf_op jit(solution)/shard_map/all_gather | solution.py:52
  145.6 4.9 %multiply_subtract_fusion = (f32[128,4096]{1,0:T(8,128)}, f32[128,4096]{1,0:T(8,128)}) fusion(f32[128,4096]{1,0:T(8,128)S(1)} %copy-done, f32[128,4096]{1,0:T(8,128)} %all-gather.2.cloned.1.call-done, f32[]{:T(128)S(6)} %min_shard_map.3, f32[128,4096]{1,0:T(8,128)} %param.5), kind=kLoop, calls=%fused_computation.2 | loop fusion | flops 3670016 | bytes 10485764 | tf_op jit(solution)/shard_map/sub | solution.py:55
  (6 shorter events, 0.0 us)
Async XLA Ops:
  9.7 40.6 %copy-start.1 = (bf16[1,128,4096]{2,1,0:T(8,128)(2,1)S(1)}, bf16[1,128,4096]{2,1,0:T(8,128)(2,1)}, u32[]{:S(2)}) copy-start(bf16[1,128,4096]{2,1,0:T(8,128)(2,1)} %param.4) | copy-start | bytes 3145732
  71.4 22.5 %all-to-all-start = ((bf16[8,1,16,4096]{3,2,1,0:T(8,128)(2,1)}), bf16[8,1,16,4096]{3,2,1,0:T(8,128)(2,1)S(1)}, u32[]{:S(2)}, u32[]{:S(2)}) async-start(bf16[8,1,16,4096]{3,2,1,0:T(8,128)(2,1)} %fusion.1), calls=%async_computation | async-start | bytes 2097152 | tf_op jit(solution)/shard_map/all_to_all | solution.py:40
  75.0 70.6 %all-gather.2.cloned.1.call-start = ((), (), s32[]{:S(2)}) async-start(), calls=%async_computation.1 | async-start | bytes 2359296 | tf_op jit(solution)/shard_map/all_gather | solution.py:52
  78.0 67.6 %copy-start = (f32[128,4096]{1,0:T(8,128)S(1)}, f32[128,4096]{1,0:T(8,128)}, u32[]{:S(2)}) copy-start(f32[128,4096]{1,0:T(8,128)} %param.3) | copy-start | bytes 6291460
Sparse Core Ops, SparseCore 0:
  96.5 49.0 all-gather.1

commit v2 on v0

--- a/solution.py
+++ b/solution.py
@@ -44,7 +44,10 @@
     entry_count = row_count * lax.axis_size("shard") * col_count
     root_mean = jnp.sqrt(square_total / entry_count + epsilon)
     factor = jnp.minimum(1.0, clip_level / root_mean)
-    gradient = lax.all_gather(gradient_slice, "replica", axis=0, tiled=True)
+    gradient = jnp.concatenate(
+        lax.all_to_all(jnp.stack([gradient_slice] * lax.axis_size("replica")), "replica", 0, 0),
+        axis=0,
+    )
     clipped = factor * gradient
     momentum_next = outer_decay * momentum + clipped
     params_next = outer_params - outer_rate * (clipped + outer_decay * momentum_next)

time: 172 us -> 188 us (1.093)
  blocking collectives: 78.7 us -> 104 us
  between operations: 14.8 us -> 1.43 us
  waiting for transfers between devices: 24.3 us -> 14 us
  local copies, waits for them, and re-layouts: 14.4 us -> 24.5 us
  starting transfers between devices: 3.78 us -> 8.08 us
    psum x1, blocking collectives: 39.4 us -> 64.2 us  [per_device(): lax.psum(jnp.sum(gradient_slice * gradient_slice), ('replica', 'shard'))]
    unnamed x11 -> x15, local copies, waits for them, and re-layouts: 10.1 us -> 18.7 us
    all_gather x1 -> x0, waiting for transfers between devices: 8.49 us -> none  [per_device(): gradient = lax.all_gather(gradient_slice, 'replica', axis=0, tiled=True)]
    all_to_all x0 -> x1, starting transfers between devices: none -> 4.34 us  [per_device(): lax.all_to_all(jnp.stack([gradient_slice] * lax.axis_size('replica')), 'r...]
    sub x1, other arithmetic: 4.9 us -> 2.84 us  [per_device(): outer_params - outer_rate * (clipped + outer_decay * momentum_next)]
    mul x0 -> x1, other arithmetic: none -> 1.91 us  [per_device(): clipped = factor * gradient]
  transfers between devices with their start and end apart: 2 -> 2, of which waited for: 2 -> 1; matrix products, arithmetic and copies ran while one was open for 2% -> 3% of each run, Pallas kernels for 0% -> 0%
where the time goes in v2:
time: 188 us; the launch traced here: 187 us
  blocking collectives  104 us (55%)
  other arithmetic  35.8 us (19%)
  local copies, waits for them, and re-layouts  24.5 us (13%)
  waiting for transfers between devices  14 us (7%)
  starting transfers between devices  8.08 us (4%)
    psum x1, blocking collectives, per_device(): lax.psum(jnp.sum(gradient_slice * gradient_slice), ('replica', 'shard'))  64.2 us
    pmax x1, blocking collectives, per_device(): absmax = lax.pmax(block_max(deltas), 'replica')  39.3 us
    unnamed x15, local copies, waits for them, and re-layouts  18.7 us
    broadcast_in_dim x1, other arithmetic, per_device(): encoded[None]  14.9 us
    all_to_all x1, waiting for transfers between devices, per_device(): lax.all_to_all(encoded[None], 'replica', split_axis=1, concat_axis=0, til...  14 us
    unnamed x2, other arithmetic  10.5 us
    all_to_all x1, starting transfers between devices, per_device(): lax.all_to_all(jnp.stack([gradient_slice] * lax.axis_size('replica')), 'r...  4.34 us
  transfers between devices with their start and end apart: 2, of which 1 were waited for; matrix products, arithmetic and copies ran while one was open for 3% of the time, Pallas kernels for 0%

profile of v2, /device:TPU:0, one launch (start us, length us, event | category | flops | bytes accessed | tf_op | source)
XLA Modules:
  0.0 187.4 jit_solution(12963420851941670942)
XLA Ops:
  0.6 2.1 %abs_bitcast_fusion = f32[16,8,32,128]{3,1,2,0:T(8,128)S(1)} fusion(f32[128,4096]{1,0:T(8,128)} %param.3, bf16[1,128,4096]{2,1,0:T(8,128)(2,1)} %param.4), kind=kLoop, calls=%fused_computation.7 | loop fusion | flops 1572864 | bytes 5242880
  2.7 1.7 copy.11
  4.4 2.4 %reduce_max.9 = f32[128,32]{1,0:T(8,128)S(1)} reduce(f32[128,32,128]{2,1,0:T(8,128)} %bitcast.35, f32[]{:T(128)} %constant.9.clone.1), dimensions={2}, to_apply=%region_0.0 | reduce | flops 520192 | bytes 2113540 | tf_op jit(solution)/shard_map/reduce_max | solution.py:24
  6.8 39.3 %pmax.7 = f32[128,32]{1,0:T(8,128)S(1)} all-reduce(f32[128,32]{1,0:T(8,128)S(1)} %reduce_max.9), channel_id=1, replica_groups=mesh['replica'=8,'shard'=4] {'replica'}, use_global_device_ids=true, to_apply=%region_1.0 | all-reduce | flops 4096 | bytes 32768 | tf_op jit(solution)/shard_map/pmax | solution.py:36
  46.1 0.6 broadcast_in_dim.6
  46.8 1.3 copy-done.1
  48.1 14.9 %fusion.2 = bf16[1,128,4096]{2,1,0:T(8,128)(2,1)S(1)} fusion(f32[128,4096]{1,0:T(8,128)S(1)} %copy-done, bf16[1,128,4096]{2,1,0:T(8,128)(2,1)S(1)} %copy-done.2, f32[16,8,32,128]{3,2,1,0:T(8,128)S(1)} %bitcast.31), kind=kLoop, calls=%fused_computation.9 | loop fusion | flops 5767168 | bytes 6291456 | tf_op jit(solution)/shard_map/broadcast_in_dim | solution.py:39
  62.9 3.7 %copy.18 = bf16[1,128,4096]{2,0,1:T(2,128)(2,1)} copy(bf16[1,128,4096]{2,1,0:T(8,128)(2,1)S(1)} %fusion.2) | data formatting | bytes 2097152 | tf_op jit(solution)/shard_map/broadcast_in_dim | solution.py:39
  66.6 0.5 broadcast.29
  67.1 8.4 %reduce = bf16[128,4096]{1,0:T(8,128)(2,1)S(1)} reduce(bf16[128,1,4096]{2,1,0:T(2,128)(2,1)} %bitcast.34, bf16[]{:T(256)} %broadcast.29), dimensions={1}, to_apply=%bitcast.30.reduce_sub_computation | reduce | bytes 2097154
  75.5 1.6 reshape.28
  77.1 3.7 %all-to-all-start = ((bf16[8,2,32768]{2,1,0:T(2,128)(2,1)}), bf16[8,2,32768]{2,1,0:T(2,128)(2,1)S(1)}, u32[]{:S(2)}, u32[]{:S(2)}) async-start(bf16[8,2,32768]{2,1,0:T(2,128)(2,1)} %reshape.28), calls=%async_computation | async-start | bytes 2097152 | tf_op jit(solution)/shard_map/all_to_all | solution.py:39
  80.9 4.6 %copy.17 = f32[16,8,32,128]{3,1,2,0:T(8,128)} copy(f32[16,8,32,128]{3,2,1,0:T(8,128)} %bitcast.32) | data formatting | bytes 4194304
  85.4 14.0 %all-to-all-done = bf16[8,2,32768]{2,1,0:T(2,128)(2,1)S(1)} async-done(((bf16[8,2,32768]{2,1,0:T(2,128)(2,1)}), bf16[8,2,32768]{2,1,0:T(2,128)(2,1)S(1)}, u32[]{:S(2)}, u32[]{:S(2)}) %all-to-all-start) | async-done | bytes 1048608 | tf_op jit(solution)/shard_map/all_to_all | solution.py:39
  99.5 3.4 %reshape.29 = bf16[128,1,4096]{2,1,0:T(2,128)(2,1)} reshape(bf16[8,2,32768]{2,1,0:T(2,128)(2,1)S(1)} %all-to-all-done) | data formatting | bytes 2097152
  102.9 4.6 %copy.10 = f32[1,128,4096]{2,1,0:T(8,128)} copy(bf16[1,128,4096]{2,0,1:T(2,128)(2,1)} %bitcast.36) | data formatting | bytes 3145728
  107.5 1.7 reduce_sum.18
  109.2 1.6 multiply_reduce_fusion
  110.8 1.5 stack.2
  112.3 4.3 %all-to-all-start.1 = ((f32[8,16,4096]{2,1,0:T(8,128)}), f32[8,16,4096]{2,1,0:T(8,128)}, u32[]{:S(2)}, u32[]{:S(2)}) async-start(f32[8,16,4096]{2,1,0:T(8,128)} %stack.2), calls=%async_computation.1 | async-start | bytes 4194304 | tf_op jit(solution)/shard_map/all_to_all | solution.py:48
  116.7 0.7 copy.9
  117.4 64.2 %psum.7 = f32[]{:T(128)} all-reduce(f32[]{:T(128)} %get-tuple-element.11), channel_id=1, replica_groups=mesh['replica'=8,'shard'=4] {'replica','shard'}, use_global_device_ids=true, to_apply=%region_4.0 | all-reduce | flops 1 | bytes 8 | tf_op jit(solution)/shard_map/psum | solution.py:43
  182.3 1.9 %broadcast_multiply_fusion = f32[8,16,4096]{2,1,0:T(8,128)S(1)} fusion(f32[8,16,4096]{2,1,0:T(8,128)} %all-to-all-done.1, f32[]{:T(128)S(6)} %min_shard_map.3), kind=kLoop, calls=%fused_computation.8 | loop fusion | flops 524288 | bytes 4194308 | tf_op jit(solution)/shard_map/mul | solution.py:51
  184.5 2.8 %fusion.1 = (f32[128,4096]{1,0:T(8,128)}, f32[128,4096]{1,0:T(8,128)}) fusion(f32[128,4096]{1,0:T(8,128)S(1)} %copy-done, f32[8,16,4096]{2,1,0:T(8,128)S(1)} %broadcast_multiply_fusion, f32[128,4096]{1,0:T(8,128)S(1)} %copy-done.3), kind=kLoop, calls=%fused_computation.5 | loop fusion | flops 3145728 | bytes 10485760 | tf_op jit(solution)/shard_map/sub | solution.py:53
  (9 shorter events, 0.3 us)
Async XLA Ops:
  4.4 43.6 %copy-start = (f32[128,4096]{1,0:T(8,128)S(1)}, f32[128,4096]{1,0:T(8,128)}, u32[]{:S(2)}) copy-start(f32[128,4096]{1,0:T(8,128)} %param.3) | copy-start | bytes 6291460
  4.4 43.6 %copy-start.2 = (bf16[1,128,4096]{2,1,0:T(8,128)(2,1)S(1)}, bf16[1,128,4096]{2,1,0:T(8,128)(2,1)}, u32[]{:S(2)}) copy-start(bf16[1,128,4096]{2,1,0:T(8,128)(2,1)} %param.4) | copy-start | bytes 3145732
  46.7 1.3 copy-start.1
  77.1 22.3 %all-to-all-start = ((bf16[8,2,32768]{2,1,0:T(2,128)(2,1)}), bf16[8,2,32768]{2,1,0:T(2,128)(2,1)S(1)}, u32[]{:S(2)}, u32[]{:S(2)}) async-start(bf16[8,2,32768]{2,1,0:T(2,128)(2,1)} %reshape.28), calls=%async_computation | async-start | bytes 2097152 | tf_op jit(solution)/shard_map/all_to_all | solution.py:39
  112.3 70.0 %all-to-all-start.1 = ((f32[8,16,4096]{2,1,0:T(8,128)}), f32[8,16,4096]{2,1,0:T(8,128)}, u32[]{:S(2)}, u32[]{:S(2)}) async-start(f32[8,16,4096]{2,1,0:T(8,128)} %stack.2), calls=%async_computation.1 | async-start | bytes 4194304 | tf_op jit(solution)/shard_map/all_to_all | solution.py:48
  182.3 2.2 %copy-start.3 = (f32[128,4096]{1,0:T(8,128)S(1)}, f32[128,4096]{1,0:T(8,128)}, u32[]{:S(2)}) copy-start(f32[128,4096]{1,0:T(8,128)} %param.5) | copy-start | bytes 6291460
